TPU v7x, 32 devices: a whole 2x2x4 slice. The times are simulated.
32 devices in a mesh: pool: 4 (over y, core), ga: 8 (over z, x).
Axes of the slice: x: 2, y: 2, z: 4, core: 2. Of those that a mesh axis runs over, the one named last changes fastest.
Arguments:
- coefficients: bfloat16 [4, 256, 2, 256, 128], P('pool', 'ga'), may hold values from -6 to 6
- stick_count: int32 [4, 8], P('pool', 'ga'), may hold values from 28 to 32, as said below
- dest_device: int32 [4, 256], P('pool', 'ga'), may hold values from -1 to 7, as said below
- dest_slot: int32 [4, 256], P('pool', 'ga'), may hold values from -1 to 31, as said below
- source_stick: int32 [4, 256], P('pool', 'ga'), may hold values from -1 to 255, as said below
Outputs:
- margins: float32 [4, 2, 256, 256], P('pool', None, 'ga')
Inputs may be any that keep to these rules, and one draw needn't show every extreme that they name: Every k-point has a device whose 32 slots are all live; a device's live sticks are its first stick_count slots. `dest_device`: -1 exactly for sticks that land nowhere (among them all sticks that are not live); no device sends more than 8 of its sticks to one device, and some pair of devices reaches 8 for every k-point. `dest_slot`: -1 where dest_device is -1; the slots named are live slots of the layout of k-point q-1, no slot named twice. `source_stick`: the exact inverse of dest_device and dest_slot: a slot names a stick exactly when that stick names the slot, else -1.
All inputs are finite; a program needn't handle non-finite values.
Results may differ from a plain program's by a relative error of at most 0.0003.
Values may be sent and summed in bfloat16 or wider, within the bound.
A program may use at most 64 MiB of HBM per device.

v0:
```python
import jax
import jax.numpy as jnp
from jax import lax
from jax.sharding import PartitionSpec as P


def passed_along(value, axis, steps):
    count = lax.axis_size(axis)
    pairs = [(source, (source + steps) % count) for source in range(count)]
    return lax.ppermute(value, axis, pairs)


def margin(bra_rows, ket_rows, slot_count, bands, plane_waves):
    bra_block = bra_rows.reshape(slot_count, 2, bands, plane_waves)
    ket_block = ket_rows.reshape(slot_count, 2, bands, plane_waves)
    swapped = jnp.stack([ket_block[:, 1], -ket_block[:, 0]], axis=1)
    real_part = jnp.einsum(
        "scmg,scng->mn", bra_block, ket_block, preferred_element_type=jnp.float32
    )
    imag_part = jnp.einsum("scmg,scng->mn", bra_block, swapped, preferred_element_type=jnp.float32)
    return jnp.stack([real_part, imag_part])


def owner_rows(partial_value, groups, bands, norm_scale):
    row_count = bands // groups
    totals = lax.psum(partial_value, "ga")
    owned = lax.dynamic_slice_in_dim(totals, lax.axis_index("ga") * row_count, row_count, 1)
    return owned * norm_scale


def local(coefficients, stick_count, dest_device, dest_slot, source_stick):
    groups = lax.axis_size("ga")
    slot_count = coefficients.shape[1]
    bands = coefficients.shape[3]
    plane_waves = coefficients.shape[4]
    pair_cap = max(2, (2 * slot_count + groups - 1) // groups)
    buffer_rows = groups * pair_cap
    norm_scale = (2 * groups * slot_count * plane_waves) ** (-0.5)
    coef_rows = coefficients.reshape(slot_count, -1)
    slot_list = jnp.arange(slot_count, dtype=jnp.int32)
    buffer_list = jnp.arange(buffer_rows, dtype=jnp.int32)
    live_mask = slot_list < stick_count[0, 0]
    bra_rows = jnp.where(live_mask[:, None], coef_rows, jnp.zeros_like(coef_rows))
    targets = dest_device[0]
    dest_order = dest_slot[0]
    matching = targets[:, None] == targets[None, :]
    earlier = dest_order[None, :] < dest_order[:, None]
    ranking = jnp.sum((matching & earlier).astype(jnp.int32), axis=1)
    position = jnp.where(targets >= 0, targets * pair_cap + ranking, -1)
    packer = (buffer_list[:, None] == position[None, :]).astype(jnp.bfloat16)
    outgoing = jnp.dot(packer, coef_rows, preferred_element_type=jnp.float32).astype(jnp.bfloat16)
    outgoing = outgoing.reshape(groups, pair_cap, -1)
    incoming = lax.all_to_all(outgoing, "ga", split_axis=0, concat_axis=0, tiled=True)
    anchor = source_stick[0]
    source_dev = jnp.where(anchor >= 0, anchor // slot_count, -1)
    matching_in = source_dev[:, None] == source_dev[None, :]
    earlier_in = slot_list[None, :] < slot_list[:, None]
    ranking_in = jnp.sum((matching_in & earlier_in).astype(jnp.int32), axis=1)
    position_in = jnp.where(anchor >= 0, source_dev * pair_cap + ranking_in, -1)
    placer = (position_in[:, None] == buffer_list[None, :]).astype(jnp.bfloat16)
    ket_rows = jnp.dot(
        placer, incoming.reshape(buffer_rows, -1), preferred_element_type=jnp.float32
    ).astype(jnp.bfloat16)
    bra_here = passed_along(bra_rows, "pool", 1)
    partial_value = margin(bra_here, ket_rows, slot_count, bands, plane_waves)
    finished = owner_rows(partial_value, groups, bands, norm_scale)
    result = passed_along(finished, "pool", -1)
    return result[None]


def solution(mesh):
    return jax.shard_map(
        local,
        mesh=mesh,
        in_specs=(
            P("pool", "ga", None, None, None),
            P("pool", "ga"),
            P("pool", "ga"),
            P("pool", "ga"),
            P("pool", "ga"),
        ),
        out_specs=P("pool", None, "ga", None),
        check_vma=False,
    )
```

profile of v0, /device:TPU:1, one launch (start us, length us, event | category | flops | bytes accessed | tf_op | source)
XLA Modules:
  0.0 305.1 jit_solution(17752583700953156419)
XLA Ops:
  6.5 5.6 %reshape.71 = bf16[32,65536]{1,0:T(8,128)(2,1)} reshape(bf16[1,32,2,256,128]{4,3,2,1,0:T(8,128)(2,1)} %param.5) | data formatting | bytes 8388608 | tf_op jit(solution)/shard_map/reshape | solution.py:39
  12.1 0.2 convert_reduce_fusion
  12.3 7.7 %fusion = bf16[8,8,65536]{2,1,0:T(8,128)(2,1)} fusion(bf16[32,65536]{1,0:T(8,128)(2,1)} %reshape.71, s32[32]{0:T(128)S(1)} %fusion.23), kind=kOutput, calls=%fused_computation.1 | convolution fusion | flops 272631808 | bytes 12583040 | tf_op jit(solution)/shard_map/dot_general | solution.py:51
  20.0 6.3 %all-to-all-start = ((bf16[8,8,65536]{2,1,0:T(8,128)(2,1)}), bf16[8,8,65536]{2,1,0:T(8,128)(2,1)}, u32[]{:S(2)}, u32[]{:S(2)}) async-start(bf16[8,8,65536]{2,1,0:T(8,128)(2,1)} %fusion), calls=%async_computation | async-start | bytes 16777216 | tf_op jit(solution)/shard_map/all_to_all | solution.py:53
  26.4 0.0 all-reduce.2.cloned.1.call-start
  27.1 2.5 broadcast_select_fusion
  29.6 2.1 collective-permute-start
  31.8 0.2 convert_reduce_fusion.1
  32.0 45.2 %collective-permute-done = bf16[32,65536]{1,0:T(8,128)(2,1)S(1)} collective-permute-done((bf16[32,65536]{1,0:T(8,128)(2,1)S(1)}, bf16[32,65536]{1,0:T(8,128)(2,1)S(1)}, u32[]{:S(2)}, u32[]{:S(2)}) %collective-permute-start) | collective-permute-done | bytes 4194336 | tf_op jit(solution)/shard_map/ppermute | solution.py:10
  77.2 2.9 copy.21
  80.1 128.7 %all-to-all-done = bf16[8,8,65536]{2,1,0:T(8,128)(2,1)} async-done(((bf16[8,8,65536]{2,1,0:T(8,128)(2,1)}), bf16[8,8,65536]{2,1,0:T(8,128)(2,1)}, u32[]{:S(2)}, u32[]{:S(2)}) %all-to-all-start) | async-done | bytes 8388640 | tf_op jit(solution)/shard_map/all_to_all | solution.py:53
  208.7 4.7 %fusion.9 = bf16[4,8,512,128]{3,1,2,0:T(8,128)(2,1)S(1)} fusion(bf16[8,8,65536]{2,1,0:T(8,128)(2,1)} %all-to-all-done, s32[32]{0:T(128)S(1)} %compare_select_fusion.8), kind=kOutput, calls=%fused_computation.12 | convolution fusion | flops 270534656 | bytes 12583040 | tf_op jit(solution)/shard_map/dot_general | solution.py:61
  213.4 1.0 copy.22
  214.4 0.8 fusion.27
  215.2 1.4 copy-done
  216.6 1.3 fusion.12
  217.9 1.3 fusion.15
  219.1 0.8 pad_maximum_fusion
  220.0 0.0 all-reduce.2.cloned.1.call-update
  220.0 71.4 %all-reduce.2.cloned.1.call-done = f32[2,256,256]{2,1,0:T(8,128)} async-done(((f32[2,256,256]{2,1,0:T(8,128)}), f32[2,256,256]{2,1,0:T(8,128)}) %all-reduce.2.cloned.1.call-update) | async-done | bytes 524304 | tf_op jit(solution)/shard_map/psum | solution.py:26
  291.4 0.8 dynamic-slice_multiply_fusion
  292.2 2.4 collective-permute-start.1
  294.6 3.0 collective-permute-done.1
  297.6 0.6 copy.38
  (12 shorter events, 0.1 us)
Async XLA Ops:
  6.5 5.6 %copy-start.2 = (s32[1,32]{1,0:T(1,128)S(1)}, s32[1,32]{1,0:T(1,128)}, u32[]{:S(2)}) copy-start(s32[1,32]{1,0:T(1,128)} %param.7) | copy-start | bytes 388
  6.5 5.6 %copy-start.1 = (s32[1,32]{1,0:T(1,128)S(1)}, s32[1,32]{1,0:T(1,128)}, u32[]{:S(2)}) copy-start(s32[1,32]{1,0:T(1,128)} %param.8) | copy-start | bytes 388
  20.0 188.7 %all-to-all-start = ((bf16[8,8,65536]{2,1,0:T(8,128)(2,1)}), bf16[8,8,65536]{2,1,0:T(8,128)(2,1)}, u32[]{:S(2)}, u32[]{:S(2)}) async-start(bf16[8,8,65536]{2,1,0:T(8,128)(2,1)} %fusion), calls=%async_computation | async-start | bytes 16777216 | tf_op jit(solution)/shard_map/all_to_all | solution.py:53
  26.4 265.0 %all-reduce.2.cloned.1.call-start = ((), (), s32[]{:S(2)}) async-start(), calls=%async_computation.1 | async-start | bytes 1048576 | tf_op jit(solution)/shard_map/psum | solution.py:26
  27.1 4.7 %copy-start.3 = (s32[1,32]{1,0:T(1,128)S(1)}, s32[1,32]{1,0:T(1,128)}, u32[]{:S(2)}) copy-start(s32[1,32]{1,0:T(1,128)} %param.9) | copy-start | bytes 388
  29.6 47.6 %collective-permute-start = (bf16[32,65536]{1,0:T(8,128)(2,1)S(1)}, bf16[32,65536]{1,0:T(8,128)(2,1)S(1)}, u32[]{:S(2)}, u32[]{:S(2)}) collective-permute-start(bf16[32,65536]{1,0:T(8,128)(2,1)S(1)} %broadcast_select_fusion), channel_id=1, source_target_pairs={{0,8},{8,16},{16,24},{24,0},{1,9},{9,17},{17,25},{25,1},{2,10},{10... | collective-permute-start | bytes 12582920 | tf_op jit(solution)/shard_map/ppermute | solution.py:10
  214.4 2.2 copy-start
  292.2 5.4 %collective-permute-start.1 = (f32[2,32,256]{2,1,0:T(8,128)S(1)}, f32[2,32,256]{2,1,0:T(8,128)S(1)}, u32[]{:S(2)}, u32[]{:S(2)}) collective-permute-start(f32[2,32,256]{2,1,0:T(8,128)S(1)} %dynamic-slice_multiply_fusion), channel_id=1, source_target_pairs={{0,24},{8,0},{16,8},{24,16},{1,25},{9,1},{17,9},{25,17},{2,26},{10... | collective-permute-start | bytes 196616 | tf_op jit(solution)/shard_map/ppermute | solution.py:10
Sparse Core Ops, SparseCore 0:
  220.1 71.2 all-reduce.1
where the time goes:
time: 306 us; the launch traced here: 305 us
  waiting for transfers between devices  248 us (81%)
  matrix products  15 us (5%)
  between operations  14.1 us (5%)
  local copies, waits for them, and re-layouts  11.5 us (4%)
  starting transfers between devices  10.9 us (4%)
  other arithmetic  5.37 us (2%)
    all_to_all x1, waiting for transfers between devices, local(): lax.all_to_all(outgoing, 'ga', split_axis=0, concat_axis=0, tiled=True)  129 us
    psum x1, waiting for transfers between devices, owner_rows(): totals = lax.psum(partial_value, 'ga')  71.4 us
    ppermute x2, waiting for transfers between devices, passed_along(): return lax.ppermute(value, axis, pairs)  48.2 us
    dot_general x1, matrix products, local(): jnp.dot(packer, coef_rows, preferred_element_type=jnp.float32)  7.73 us
    all_to_all x1, starting transfers between devices, local(): lax.all_to_all(outgoing, 'ga', split_axis=0, concat_axis=0, tiled=True)  6.34 us
  transfers between devices with their start and end apart: 4, of which 4 were waited for; matrix products, arithmetic and copies ran while one was open for 2% of the time, Pallas kernels for 0%

commit v1 on v0

v1 whole, which is shorter than its diff:
```python
import jax
import jax.numpy as jnp
from jax import lax
from jax.sharding import PartitionSpec as P


def passed_along(value, axis, steps):
    count = lax.axis_size(axis)
    pairs = [(source, (source + steps) % count) for source in range(count)]
    return lax.ppermute(value, axis, pairs)


def local(coefficients, stick_count, dest_device, dest_slot, source_stick):
    groups = lax.axis_size("ga")
    slot_count = coefficients.shape[1]
    bands = coefficients.shape[3]
    plane_waves = coefficients.shape[4]
    width = plane_waves // groups
    sticks = groups * slot_count
    norm_scale = (2 * groups * slot_count * plane_waves) ** (-0.5)
    split = coefficients[0].reshape(slot_count, 2, bands, groups, width)
    split = split.transpose(3, 0, 1, 4, 2)
    mine = lax.all_to_all(split, "ga", split_axis=0, concat_axis=0, tiled=True)
    mine = mine.reshape(sticks, 2 * width * bands)
    theirs = passed_along(mine, "pool", -1)
    anchor = passed_along(source_stick[0], "pool", -1)
    slot_list = jnp.arange(slot_count, dtype=jnp.int32)
    anchor = jnp.where(slot_list < stick_count[0, 0], anchor, -1)
    anchors = lax.all_gather(anchor, "ga", tiled=True)
    placer = (anchors[:, None] == jnp.arange(sticks, dtype=jnp.int32)[None, :]).astype(jnp.bfloat16)
    ket = jnp.dot(placer, theirs, preferred_element_type=jnp.float32).astype(jnp.bfloat16)
    bra = mine.reshape(sticks, 2, width, bands)
    ket = ket.reshape(sticks, 2, width, bands)
    swapped = jnp.stack([ket[:, 1], -ket[:, 0]], axis=1)
    real_part = jnp.einsum("scgm,scgn->mn", bra, ket, preferred_element_type=jnp.float32)
    imag_part = jnp.einsum("scgm,scgn->mn", bra, swapped, preferred_element_type=jnp.float32)
    partial_value = jnp.stack([real_part, imag_part])
    owned = lax.psum_scatter(partial_value, "ga", scatter_dimension=1, tiled=True)
    return (owned * norm_scale)[None]


def solution(mesh):
    return jax.shard_map(
        local,
        mesh=mesh,
        in_specs=(
            P("pool", "ga", None, None, None),
            P("pool", "ga"),
            P("pool", "ga"),
            P("pool", "ga"),
            P("pool", "ga"),
        ),
        out_specs=P("pool", None, "ga", None),
        check_vma=False,
    )
```

time: 306 us -> 293 us (0.958)
  waiting for transfers between devices: 248 us -> 118 us
  blocking collectives: 0 us -> 105 us
  local copies, waits for them, and re-layouts: 11.5 us -> 34.7 us
  starting transfers between devices: 10.9 us -> 1.86 us
    all_to_all x1 -> x0, waiting for transfers between devices: 129 us -> none  [local(): lax.all_to_all(outgoing, 'ga', split_axis=0, concat_axis=0, tiled=True)]
    all_to_all x0 -> x1, blocking collectives: none -> 98.5 us  [local(): mine = lax.all_to_all(split, 'ga', split_axis=0, concat_axis=0, tiled=True)]
    unnamed x1 -> x2, waiting for transfers between devices: 0.02 us -> 71.7 us
    psum x1 -> x0, waiting for transfers between devices: 71.4 us -> none  [owner_rows(): totals = lax.psum(partial_value, 'ga')]
    unnamed x11 -> x16, local copies, waits for them, and re-layouts: 5.9 us -> 15.6 us
    all_to_all x1 -> x0, starting transfers between devices: 6.34 us -> none  [local(): lax.all_to_all(outgoing, 'ga', split_axis=0, concat_axis=0, tiled=True)]
    unnamed x0 -> x1, blocking collectives: none -> 6.27 us
    all_to_all x0 -> x1, local copies, waits for them, and re-layouts: none -> 4.63 us  [local(): mine = lax.all_to_all(split, 'ga', split_axis=0, concat_axis=0, tiled=True)]
  transfers between devices with their start and end apart: 4 -> 3, of which waited for: 4 -> 2; matrix products, arithmetic and copies ran while one was open for 2% -> 2% of each run, Pallas kernels for 0% -> 0%
where the time goes in v1:
time: 293 us; the launch traced here: 290 us
  waiting for transfers between devices  118 us (40%)
  blocking collectives  105 us (36%)
  local copies, waits for them, and re-layouts  34.7 us (12%)
  between operations  15.4 us (5%)
  matrix products  13.3 us (5%)
    all_to_all x1, blocking collectives, local(): mine = lax.all_to_all(split, 'ga', split_axis=0, concat_axis=0, tiled=True)  98.5 us
    unnamed x2, waiting for transfers between devices  71.7 us
    ppermute x2, waiting for transfers between devices, passed_along(): return lax.ppermute(value, axis, pairs)  45.8 us
    unnamed x16, local copies, waits for them, and re-layouts  15.6 us
    reshape x1, local copies, waits for them, and re-layouts, local(): mine = mine.reshape(sticks, 2 * width * bands)  7.46 us
    unnamed x1, blocking collectives  6.27 us
  transfers between devices with their start and end apart: 3, of which 2 were waited for; matrix products, arithmetic and copies ran while one was open for 2% of the time, Pallas kernels for 0%

profile of v1, /device:TPU:1, one launch (start us, length us, event | category | flops | bytes accessed | tf_op | source)
XLA Modules:
  0.0 290.3 jit_solution(12320744381638329424)
XLA Ops:
  6.5 6.5 %copy.16 = bf16[1,32,2,256,128]{3,4,2,1,0:T(8,128)(2,1)} copy(bf16[1,32,2,256,128]{4,3,2,1,0:T(8,128)(2,1)} %param.5) | data formatting | bytes 8388608 | tf_op args[0]
  13.0 2.8 copy.17
  15.8 98.5 %all_to_all.5 = bf16[8,32,2,16,256]{4,3,2,1,0:T(8,128)(2,1)} all-to-all(bf16[8,32,2,16,256]{4,3,2,1,0:T(8,128)(2,1)S(1)} %copy.17), channel_id=1, replica_groups=mesh['pool'=4,'ga'=8] {'ga'}, dimensions={0} | all-to-all | bytes 8388608 | tf_op jit(solution)/shard_map/all_to_all | solution.py:23
  114.4 7.5 %reshape.7 = bf16[256,8192]{1,0:T(8,128)(2,1)} reshape(bf16[8,32,2,16,256]{4,3,2,1,0:T(8,128)(2,1)} %all_to_all.5) | data formatting | bytes 8388608 | tf_op jit(solution)/shard_map/reshape | solution.py:24
  121.8 1.9 collective-permute-start.1
  124.4 0.6 fusion.20
  125.5 45.8 %collective-permute-done = s32[32]{0:T(128)S(1)} collective-permute-done((s32[32]{0:T(128)S(1)}, s32[32]{0:T(128)S(1)}, u32[]{:S(2)}, u32[]{:S(2)}) %collective-permute-start) | collective-permute-done | bytes 160 | tf_op jit(solution)/shard_map/ppermute | solution.py:10
  171.3 0.1 fusion.17
  171.4 6.3 %all-reduce = s32[256]{0:T(256)S(1)} all-reduce(s32[256]{0:T(256)S(1)} %fusion.17), channel_id=1, replica_groups=mesh['pool'=4,'ga'=8] {'ga'}, use_global_device_ids=true, to_apply=%add | all-reduce | flops 256 | bytes 2048
  177.7 4.6 %copy.18 = bf16[8,32,2,16,256]{4,3,1,0,2:T(8,128)(2,1)} copy(bf16[8,32,2,16,256]{4,3,2,1,0:T(8,128)(2,1)} %all_to_all.5) | data formatting | bytes 8388608 | tf_op jit(solution)/shard_map/all_to_all | solution.py:23
  182.3 3.5 %convolution_convert_fusion = bf16[256,8192]{1,0:T(8,128)(2,1)S(1)} fusion(bf16[256,8192]{1,0:T(8,128)(2,1)} %collective-permute-done.1, s32[256]{0:T(256)S(1)} %all-reduce), kind=kOutput, calls=%fused_computation | convolution fusion | flops 1075904512 | bytes 8389632 | tf_op jit(solution)/shard_map/dot_general | solution.py:31
  185.8 1.4 copy.30
  187.2 2.5 fusion.19
  189.7 0.7 copy-done.1
  190.5 3.0 %copy.29 = bf16[256,1,16,256]{0,3,2,1:T(8,128)(2,1)S(1)} copy(bf16[256,1,16,256]{3,2,1,0:T(8,128)(2,1)} %get-tuple-element.6) | data formatting | bytes 4194304
  193.5 1.8 neg.4
  195.2 3.0 %copy.28 = bf16[256,1,16,256]{0,3,2,1:T(8,128)(2,1)S(1)} copy(bf16[256,1,16,256]{3,2,1,0:T(8,128)(2,1)} %get-tuple-element.5) | data formatting | bytes 4194304
  198.2 4.9 %fusion.7 = f32[1,256,256]{1,2,0:T(8,128)S(1)} fusion(bf16[256,2,16,256]{3,2,0,1:T(8,128)(2,1)} %bitcast.40, bf16[256,2,16,256]{3,2,1,0:T(8,128)(2,1)} %bitcast.37), kind=kOutput, calls=%fused_computation.8 | convolution fusion | flops 1073741824 | bytes 8650752 | tf_op jit(solution)/shard_map/scgm,scgn->mn/dot_general | solution.py:35
  203.1 0.4 copy-done.2
  203.6 4.9 %fusion.10 = f32[1,256,256]{1,2,0:T(8,128)S(1)} fusion(bf16[256,2,16,256]{3,2,1,0:T(8,128)(2,1)S(1)} %bitcast.35, bf16[256,1,16,256]{0,3,2,1:T(8,128)(2,1)S(1)} %copy-done.2, bf16[256,1,16,256]{0,3,2,1:T(8,128)(2,1)S(1)} %copy.28), kind=kOutput, calls=%fused_computation.9 | convolution fusion | flops 1075838976 | bytes 8650752 | tf_op jit(solution)/shard_map/scgm,scgn->mn/dot_general | solution.py:36
  208.5 1.0 copy.23
  210.2 71.7 %all-reduce.4.cloned.1.call-done = f32[2,256,256]{2,0,1:T(2,128)} async-done(((f32[2,256,256]{2,0,1:T(2,128)}), f32[2,256,256]{2,0,1:T(2,128)}) %all-reduce.4.cloned.1.call-update) | async-done | bytes 524304
  282.0 0.9 fusion.16
  282.8 0.6 copy.24
  (14 shorter events, 0.1 us)
Async XLA Ops:
  6.5 275.4 %all-reduce.4.cloned.1.call-start = ((), (), s32[]{:S(2)}) async-start(), calls=%async_computation.1 | async-start | bytes 1048576
  114.4 9.3 %copy-start.4 = (s32[1,32]{1,0:T(1,128)S(1)}, s32[1,32]{1,0:T(1,128)}, u32[]{:S(2)}) copy-start(s32[1,32]{1,0:T(1,128)} %param.7) | copy-start | bytes 388
  114.4 10.0 %copy-start.3 = (u32[32]{0:T(128)S(1)}, u32[32]{0:T(128)}, u32[]{:S(2)}) copy-start(u32[32]{0:T(128)} %constant.9) | copy-start | bytes 388
  121.8 60.5 %collective-permute-start.1 = (bf16[256,8192]{1,0:T(8,128)(2,1)}, bf16[256,8192]{1,0:T(8,128)(2,1)}, u32[]{:S(2)}, u32[]{:S(2)}) collective-permute-start(bf16[256,8192]{1,0:T(8,128)(2,1)} %reshape.7), channel_id=1, source_target_pairs={{0,24},{8,0},{16,8},{24,16},{1,25},{9,1},{17,9},{25,17},{2,26},{10... | collective-permute-start | bytes 12582920 | tf_op jit(solution)/shard_map/ppermute | solution.py:10
  123.7 47.6 %collective-permute-start = (s32[32]{0:T(128)S(1)}, s32[32]{0:T(128)S(1)}, u32[]{:S(2)}, u32[]{:S(2)}) collective-permute-start(s32[32]{0:T(128)S(1)} %bitcast.41), channel_id=1, source_target_pairs={{0,24},{8,0},{16,8},{24,16},{1,25},{9,1},{17,9},{25,17},{2,26},{10... | collective-permute-start | bytes 392 | tf_op jit(solution)/shard_map/ppermute | solution.py:10
  187.2 3.3 %copy-start.1 = (bf16[32,8,32,256]{3,2,1,0:T(8,128)(2,1)}, bf16[32,8,32,256]{3,2,1,0:T(8,128)(2,1)S(1)}, u32[]{:S(2)}) copy-start(bf16[32,8,32,256]{3,2,1,0:T(8,128)(2,1)S(1)} %copy.30) | copy-start | bytes 12582916
  198.2 4.9 %copy-start = (bf16[8,32,2,16,256]{4,3,2,1,0:T(8,128)(2,1)S(1)}, bf16[8,32,2,16,256]{4,3,2,1,0:T(8,128)(2,1)}, u32[]{:S(2)}) copy-start(bf16[8,32,2,16,256]{4,3,2,1,0:T(8,128)(2,1)} %all_to_all.5) | copy-start | bytes 12582916
  198.2 5.3 %copy-start.2 = (bf16[256,1,16,256]{0,3,2,1:T(8,128)(2,1)S(1)}, bf16[256,1,16,256]{0,3,2,1:T(8,128)(2,1)}, u32[]{:S(2)}) copy-start(bf16[256,1,16,256]{0,3,2,1:T(8,128)(2,1)} %neg.4) | copy-start | bytes 6291460
Sparse Core Ops, SparseCore 0:
  209.7 72.2 all-reduce.3

commit v2 on v1

--- a/solution.py
+++ b/solution.py
@@ -1,7 +1,275 @@
+import functools
+
 import jax
 import jax.numpy as jnp
 from jax import lax
+from jax.experimental import pallas as pl
+from jax.experimental.pallas import tpu as pltpu
 from jax.sharding import PartitionSpec as P
+
+MESH = pl.DeviceIdType.MESH
+CHUNKS = 8
+
+
+def kernel(
+    scale, coef, count, source, out,
+    stage, send, mine, theirs, ket, acc, rs, near_map, far_map, slot_map,
+    load_sem, own_sem, send_sem, recv_sem, fsend_sem, frecv_sem,
+    map_send, map_recv, fmap_send, fmap_recv, map_sem, rs_send, rs_recv,
+):
+    groups, pools = lax.axis_size("ga"), lax.axis_size("pool")
+    me, pool = lax.axis_index("ga"), lax.axis_index("pool")
+    prev, succ = lax.rem(pool + pools - 1, pools), lax.rem(pool + 1, pools)
+    slots, _, bands, waves = stage.shape
+    width = waves // groups
+    depth = 2 * width
+    part = slots // CHUNKS
+    half = bands // 2
+    rows = bands // groups
+
+    def load(c):
+        span = pl.ds(c * part, part)
+        return pltpu.make_async_copy(coef.at[0, span], stage.at[span], load_sem.at[c])
+
+    def own(c):
+        return pltpu.make_async_copy(
+            send.at[me, pl.ds(c * part, part)],
+            mine.at[pl.ds(me * slots + c * part, part)],
+            own_sem.at[c],
+        )
+
+    def exchange(c, r):
+        dest = lax.rem(me + r, groups)
+        return pltpu.make_async_remote_copy(
+            src_ref=send.at[dest, pl.ds(c * part, part)],
+            dst_ref=mine.at[pl.ds(me * slots + c * part, part)],
+            send_sem=send_sem.at[c, r],
+            recv_sem=recv_sem.at[c, r],
+            device_id={"ga": dest},
+            device_id_type=MESH,
+        )
+
+    def forward(c, r):
+        origin = lax.rem(me + groups - r, groups)
+        span = pl.ds(origin * slots + c * part, part)
+        return pltpu.make_async_remote_copy(
+            src_ref=mine.at[span],
+            dst_ref=theirs.at[span],
+            send_sem=fsend_sem.at[c, r],
+            recv_sem=frecv_sem.at[c, r],
+            device_id={"pool": prev},
+            device_id_type=MESH,
+        )
+
+    def map_copy(r):
+        dest = lax.rem(me + r, groups)
+        return pltpu.make_async_remote_copy(
+            src_ref=source,
+            dst_ref=near_map.at[me],
+            send_sem=map_send.at[r],
+            recv_sem=map_recv.at[r],
+            device_id={"ga": dest},
+            device_id_type=MESH,
+        )
+
+    def map_forward():
+        return pltpu.make_async_remote_copy(
+            src_ref=near_map,
+            dst_ref=far_map,
+            send_sem=fmap_send,
+            recv_sem=fmap_recv,
+            device_id={"pool": prev},
+            device_id_type=MESH,
+        )
+
+    for c in range(CHUNKS):
+        load(c).start()
+    own_map = pltpu.make_async_copy(source, near_map.at[me], map_sem)
+    own_map.start()
+
+    barrier = pltpu.get_barrier_semaphore()
+    for r in range(1, groups):
+        pl.semaphore_signal(
+            barrier, inc=1, device_id={"ga": lax.rem(me + r, groups)}, device_id_type=MESH
+        )
+    for other in (prev, succ):
+        pl.semaphore_signal(barrier, inc=1, device_id={"pool": other}, device_id_type=MESH)
+
+    def transposed(c):
+        load(c).wait()
+        for s in range(part):
+            slot = c * part + s
+            live = slot < count[0, 0]
+            for k in range(2):
+                block = stage[slot, k]
+                block = jnp.where(live, block, jnp.zeros_like(block)).T
+                send[:, slot, k * width:(k + 1) * width, :] = block.reshape(groups, width, bands)
+
+    order = [groups // 2] + [r for d in range(1, groups // 2) for r in (groups // 2 - d, groups // 2 + d)]
+    order = order[: groups - 1]
+
+    def send_chunk(c):
+        for r in order:
+            exchange(c, r).start()
+        own(c).start()
+
+    transposed(0)
+    pl.semaphore_wait(barrier, groups + 1)
+
+    def step(c, carry):
+        transposed(c)
+        send_chunk(c - 1)
+        return carry
+
+    lax.fori_loop(1, CHUNKS, step, 0)
+    own_map.wait()
+    for r in range(1, groups):
+        map_copy(r).start()
+    send_chunk(CHUNKS - 1)
+    for r in range(1, groups):
+        map_copy(r).wait()
+    map_forward().start()
+
+    def pass_on(c, carry):
+        own(c).wait()
+        forward(c, 0).start()
+        for r in order[::-1]:
+            exchange(c, r).wait_recv()
+            forward(c, r).start()
+        return carry
+
+    lax.fori_loop(0, CHUNKS, pass_on, 0)
+    map_forward().wait()
+    to_scalar = pltpu.make_async_copy(far_map, slot_map, map_sem)
+    to_scalar.start()
+    to_scalar.wait()
+
+    def arrived(c, carry):
+        for r in range(groups):
+            forward(c, r).wait_recv()
+        return carry
+
+    lax.fori_loop(0, CHUNKS, arrived, 0)
+
+    near_half = me // (groups // 2)
+    far_half = 1 - near_half
+
+    def gather(b):
+        for s in range(slots):
+            index = slot_map[b, 0, s]
+            block = theirs[jnp.maximum(index, 0)]
+            block = jnp.where(index >= 0, block, jnp.zeros_like(block))
+            span = pl.ds((b * slots + s) * depth, depth)
+            ket[span, 0:bands] = block
+            ket[span, bands:2 * bands] = jnp.concatenate([block[width:], -block[:width]], axis=0)
+
+    def product(b, side):
+        columns = pl.ds(pl.multiple_of(side * half, half), half)
+        bra = mine[pl.ds(b * slots, slots), :, columns].reshape(slots * depth, half)
+        other = ket[pl.ds(b * slots * depth, slots * depth), :]
+        value = lax.dot_general(
+            bra, other, (((0,), (0,)), ((), ())), preferred_element_type=jnp.float32
+        )
+        span = pl.ds(side * half, half)
+        acc[span, :] += value
+
+    acc[...] = jnp.zeros_like(acc)
+
+    def far_step(b, carry):
+        gather(b)
+        product(b, far_half)
+        return carry
+
+    lax.fori_loop(0, groups, far_step, 0)
+
+    def piece(dest):
+        return pltpu.make_async_remote_copy(
+            src_ref=acc.at[pl.ds(dest * rows, rows)],
+            dst_ref=rs.at[me],
+            send_sem=rs_send.at[dest],
+            recv_sem=rs_recv.at[me],
+            device_id={"ga": dest},
+            device_id_type=MESH,
+        )
+
+    def landed(origin):
+        return pltpu.make_async_remote_copy(
+            src_ref=acc.at[pl.ds(origin * rows, rows)],
+            dst_ref=rs.at[origin],
+            send_sem=rs_send.at[origin],
+            recv_sem=rs_recv.at[origin],
+            device_id={"ga": origin},
+            device_id_type=MESH,
+        )
+
+    product(0, near_half)
+    mates = groups // 2
+    for j in range(mates):
+        piece(far_half * mates + lax.rem(me + j, mates)).start()
+
+    def near_step(b, carry):
+        product(b, near_half)
+        return carry
+
+    lax.fori_loop(1, groups, near_step, 0)
+    total = acc[pl.ds(me * rows, rows), :]
+    rs[pl.ds(me, 1)] = total[None]
+    for j in range(1, mates):
+        piece(near_half * mates + lax.rem(me + j, mates)).start()
+    for r in range(1, groups):
+        landed(lax.rem(me + r, groups)).wait_recv()
+    total = rs[0]
+    for g in range(1, groups):
+        total = total + rs[g]
+    total = total * scale
+    out[0, 0] = total[:, :bands]
+    out[0, 1] = total[:, bands:]
+
+    def drain(c, carry):
+        for r in range(groups):
+            forward(c, r).wait_send()
+        for r in range(1, groups):
+            exchange(c, r).wait_send()
+        return carry
+
+    lax.fori_loop(0, CHUNKS, drain, 0)
+    for r in range(1, groups):
+        landed(lax.rem(me + r, groups)).wait_send()
+
+
+def in_one_kernel(coefficients, stick_count, dest_device, dest_slot, source_stick):
+    groups = lax.axis_size("ga")
+    _, slots, _, bands, waves = coefficients.shape
+    depth = 2 * waves // groups
+    sticks = groups * slots
+    rows = bands // groups
+    scale = (2 * sticks * waves) ** (-0.5)
+    any_space = pl.BlockSpec(memory_space=pl.ANY)
+    sems = pltpu.SemaphoreType.DMA
+    grid_sems = sems((CHUNKS, groups))
+    return pl.pallas_call(
+        functools.partial(kernel, scale),
+        out_shape=jax.ShapeDtypeStruct((1, 2, rows, bands), jnp.float32),
+        in_specs=[any_space, pl.BlockSpec(memory_space=pltpu.SMEM), pl.BlockSpec(memory_space=pltpu.VMEM)],
+        out_specs=pl.BlockSpec(memory_space=pltpu.VMEM),
+        scratch_shapes=[
+            pltpu.VMEM((slots, 2, bands, waves), coefficients.dtype),
+            pltpu.VMEM((groups, slots, depth, bands), coefficients.dtype),
+            pltpu.VMEM((sticks, depth, bands), coefficients.dtype),
+            pltpu.VMEM((sticks, depth, bands), coefficients.dtype),
+            pltpu.VMEM((sticks * depth, 2 * bands), coefficients.dtype),
+            pltpu.VMEM((bands, 2 * bands), jnp.float32),
+            pltpu.VMEM((groups, rows, 2 * bands), jnp.float32),
+            pltpu.VMEM((groups, 1, slots), jnp.int32),
+            pltpu.VMEM((groups, 1, slots), jnp.int32),
+            pltpu.SMEM((groups, 1, slots), jnp.int32),
+            sems((CHUNKS,)), sems((CHUNKS,)),
+            grid_sems, grid_sems, grid_sems, grid_sems,
+            sems((groups,)), sems((groups,)), sems, sems, sems,
+            sems((groups,)), sems((groups,)),
+        ],
+        compiler_params=pltpu.CompilerParams(collective_id=0, has_side_effects=True, vmem_limit_bytes=60 * 1024 * 1024),
+    )(coefficients, stick_count, source_stick)
 
 
 def passed_along(value, axis, steps):
@@ -10,7 +278,7 @@
     return lax.ppermute(value, axis, pairs)
 
 
-def local(coefficients, stick_count, dest_device, dest_slot, source_stick):
+def with_collectives(coefficients, stick_count, dest_device, dest_slot, source_stick):
     groups = lax.axis_size("ga")
     slot_count = coefficients.shape[1]
     bands = coefficients.shape[3]
@@ -39,6 +307,13 @@
     return (owned * norm_scale)[None]
 
 
+def local(coefficients, *rest):
+    width = coefficients.shape[4] // lax.axis_size("ga")
+    if width % 16 == 0 and coefficients.shape[1] % CHUNKS == 0:
+        return in_one_kernel(coefficients, *rest)
+    return with_collectives(coefficients, *rest)
+
+
 def solution(mesh):
     return jax.shard_map(
         local,

time: 293 us -> 159 us (0.54)
  Pallas kernels: 0 us -> 157 us
  waiting for transfers between devices: 118 us -> 0 us
  blocking collectives: 105 us -> 0 us
  local copies, waits for them, and re-layouts: 34.7 us -> 1.47 us
  between operations: 15.4 us -> 0.66 us
  matrix products: 13.3 us -> 0 us
    pallas_call x0 -> x1, Pallas kernels: none -> 157 us  [in_one_kernel(): pl.pallas_call(functools.partial(kernel, scale), out_shape=jax.ShapeDtype...]
    all_to_all x1 -> x0, blocking collectives: 98.5 us -> none  [local(): mine = lax.all_to_all(split, 'ga', split_axis=0, concat_axis=0, tiled=True)]
    unnamed x2 -> x0, waiting for transfers between devices: 71.7 us -> none
    ppermute x2 -> x0, waiting for transfers between devices: 45.8 us -> none  [passed_along(): return lax.ppermute(value, axis, pairs)]
    unnamed x16 -> x1, local copies, waits for them, and re-layouts: 15.6 us -> 1.47 us
    dot_general x3 -> x0, matrix products: 13.3 us -> none  [the longest x1 4.94 us: local(): jnp.einsum('scgm,scgn->mn', bra, swapped, preferred_element_type=jnp.floa...]
    reshape x1 -> x0, local copies, waits for them, and re-layouts: 7.46 us -> none  [local(): mine = mine.reshape(sticks, 2 * width * bands)]
    unnamed x1 -> x0, blocking collectives: 6.27 us -> none
  transfers between devices with their start and end apart: 3 -> 0, of which waited for: 2 -> 0; matrix products, arithmetic and copies ran while one was open for 2% -> 0% of each run, Pallas kernels for 0% -> 0%
where the time goes in v2:
time: 159 us
  Pallas kernels  157 us (99%)
    pallas_call x1, Pallas kernels, in_one_kernel(): pl.pallas_call(functools.partial(kernel, scale), out_shape=jax.ShapeDtype...  157 us

profile of v2, /device:TPU:1, one launch (start us, length us, event | category | flops | bytes accessed | tf_op | source)
XLA Modules:
  0.0 158.8 jit_solution(11413989980701848680)
XLA Ops:
  0.7 156.6 %shard_map.37 = f32[1,2,32,256]{3,2,1,0:T(8,128)} custom-call(bf16[1,32,2,256,128]{4,3,2,1,0:T(8,128)(2,1)} %coef.1, s32[1,1]{1,0:T(1,128)S(6)} %copy.5.count, s32[1,32]{1,0:T(1,128)} %source.1), custom_call_target="tpu_custom_call" | custom-call | tf_op jit(solution)/shard_map/pallas_call | solution.py:250
  157.3 1.5 copy.6

commit v3 on v2

--- a/solution.py
+++ b/solution.py
@@ -9,6 +9,7 @@
 
 MESH = pl.DeviceIdType.MESH
 CHUNKS = 8
+WINDOW = 2
 
 
 def kernel(
@@ -113,32 +114,37 @@
             exchange(c, r).start()
         own(c).start()
 
-    transposed(0)
-    pl.semaphore_wait(barrier, groups + 1)
-
-    def step(c, carry):
-        transposed(c)
-        send_chunk(c - 1)
-        return carry
-
-    lax.fori_loop(1, CHUNKS, step, 0)
-    own_map.wait()
-    for r in range(1, groups):
-        map_copy(r).start()
-    send_chunk(CHUNKS - 1)
-    for r in range(1, groups):
-        map_copy(r).wait()
-    map_forward().start()
-
-    def pass_on(c, carry):
+    def pass_on(c):
         own(c).wait()
         forward(c, 0).start()
         for r in order[::-1]:
             exchange(c, r).wait_recv()
             forward(c, r).start()
-        return carry
-
-    lax.fori_loop(0, CHUNKS, pass_on, 0)
+
+    def feed(c, carry):
+        transposed(c)
+        pass_on(c - WINDOW)
+        send_chunk(c)
+        return carry
+
+    def finish(c, carry):
+        pass_on(c)
+        return carry
+
+    transposed(0)
+    pl.semaphore_wait(barrier, groups + 1)
+    for c in range(1, WINDOW):
+        transposed(c)
+        send_chunk(c - 1)
+    own_map.wait()
+    for r in range(1, groups):
+        map_copy(r).start()
+    send_chunk(WINDOW - 1)
+    lax.fori_loop(WINDOW, CHUNKS, feed, 0)
+    for r in range(1, groups):
+        map_copy(r).wait()
+    map_forward().start()
+    lax.fori_loop(CHUNKS - WINDOW, CHUNKS, finish, 0)
     map_forward().wait()
     to_scalar = pltpu.make_async_copy(far_map, slot_map, map_sem)
     to_scalar.start()

time: 159 us -> 121 us (0.76)
  Pallas kernels: 157 us -> 119 us
    pallas_call x1, Pallas kernels: 157 us -> 119 us  [in_one_kernel(): pl.pallas_call(functools.partial(kernel, scale), out_shape=jax.ShapeDtype...]
where the time goes in v3:
time: 121 us
  Pallas kernels  119 us (98%)
  local copies, waits for them, and re-layouts  1.47 us (1%)
    pallas_call x1, Pallas kernels, in_one_kernel(): pl.pallas_call(functools.partial(kernel, scale), out_shape=jax.ShapeDtype...  119 us

profile of v3, /device:TPU:1, one launch (start us, length us, event | category | flops | bytes accessed | tf_op | source)
XLA Modules:
  0.0 121.1 jit_solution(16681429191227554810)
XLA Ops:
  0.7 119.0 %shard_map.37 = f32[1,2,32,256]{3,2,1,0:T(8,128)} custom-call(bf16[1,32,2,256,128]{4,3,2,1,0:T(8,128)(2,1)} %coef.1, s32[1,1]{1,0:T(1,128)S(6)} %copy.5.count, s32[1,32]{1,0:T(1,128)} %source.1), custom_call_target="tpu_custom_call" | custom-call | tf_op jit(solution)/shard_map/pallas_call | solution.py:256
  119.6 1.5 %copy.6 = f32[1,2,32,256]{3,2,1,0:T(8,128)} copy(f32[1,2,32,256]{3,2,1,0:T(8,128)} %shard_map.37) | data formatting | bytes 131072

commit v4 on v3

--- a/solution.py
+++ b/solution.py
@@ -133,13 +133,15 @@
 
     transposed(0)
     pl.semaphore_wait(barrier, groups + 1)
+    send_chunk(0)
     for c in range(1, WINDOW):
         transposed(c)
-        send_chunk(c - 1)
     own_map.wait()
     for r in range(1, groups):
         map_copy(r).start()
-    send_chunk(WINDOW - 1)
+    for c in range(1, WINDOW):
+        send_chunk(c)
+    acc[...] = jnp.zeros_like(acc)
     lax.fori_loop(WINDOW, CHUNKS, feed, 0)
     for r in range(1, groups):
         map_copy(r).wait()
@@ -178,8 +180,6 @@
         )
         span = pl.ds(side * half, half)
         acc[span, :] += value
-
-    acc[...] = jnp.zeros_like(acc)
 
     def far_step(b, carry):
         gather(b)

time: 121 us -> 121 us (level)
  no operation moved by 1% of the time
where the time goes in v4:
time: 121 us
  Pallas kernels  119 us (98%)
  local copies, waits for them, and re-layouts  1.47 us (1%)
    pallas_call x1, Pallas kernels, in_one_kernel(): pl.pallas_call(functools.partial(kernel, scale), out_shape=jax.ShapeDtype...  119 us

profile of v4, /device:TPU:1, one launch (start us, length us, event | category | flops | bytes accessed | tf_op | source)
XLA Modules:
  0.0 120.9 jit_solution(8395296786277418716)
XLA Ops:
  0.7 118.8 %shard_map.37 = f32[1,2,32,256]{3,2,1,0:T(8,128)} custom-call(bf16[1,32,2,256,128]{4,3,2,1,0:T(8,128)(2,1)} %coef.1, s32[1,1]{1,0:T(1,128)S(6)} %copy.5.count, s32[1,32]{1,0:T(1,128)} %source.1), custom_call_target="tpu_custom_call" | custom-call | tf_op jit(solution)/shard_map/pallas_call | solution.py:256
  119.4 1.5 %copy.6 = f32[1,2,32,256]{3,2,1,0:T(8,128)} copy(f32[1,2,32,256]{3,2,1,0:T(8,128)} %shard_map.37) | data formatting | bytes 131072
